TPU v7x, 32 devices: a whole 2x2x4 slice. The times are simulated.
32 devices in a mesh: blk: 16 (over z, y, core), grp: 2 (over x).
Axes of the slice: x: 2, y: 2, z: 4, core: 2. Of those that a mesh axis runs over, the one named last changes fastest.
Arguments:
- matrix_sat: float32 [512, 65536], P('grp', 'blk'), may hold values from -0.07883404 to 0.07883404
- matrix_ter: float32 [512, 65536], P('grp', 'blk'), may hold values from -0.07883404 to 0.07883404
- probes: float32 [16, 65536], P(None, 'blk'), may hold values from -6 to 6
Outputs:
- row_part: float32 [2, 16, 512], P(None, None, 'grp')
- column_part: float32 [2, 16, 65536], P(None, None, ('blk', 'grp'))
- trace_terms: float32 [2, 16], replicated
All inputs are finite; a program needn't handle non-finite values.
Results may differ from a plain program's by a relative error of at most 0.000096.
Values sent between devices are 32-bit elements; how exact they have to be, the bound alone decides.
A program may use at most 64 MiB of HBM per device.

v0:
```python
import jax
import jax.numpy as jnp
from jax import lax
from jax.sharding import PartitionSpec as P


def broadcast(block, axis, source):
    block = jnp.where(lax.axis_index(axis) == source, block, jnp.zeros_like(block))
    return lax.psum(block, axis)


def shards(matrix_sat, matrix_ter, probes):
    rows_dev, cols_dev = matrix_sat.shape
    column_index = lax.axis_index("blk")
    row_index = lax.axis_index("grp")
    row_ids = row_index * rows_dev + lax.broadcasted_iota(jnp.int32, (rows_dev, cols_dev), 0)
    col_ids = column_index * cols_dev + lax.broadcasted_iota(jnp.int32, (rows_dev, cols_dev), 1)
    upper_mask = col_ids >= row_ids
    strict_mask = col_ids > row_ids
    mine = lax.dynamic_slice_in_dim(probes, row_index * rows_dev, rows_dev, 1)
    slab_probes = broadcast(mine, "blk", 0)
    hp = lax.Precision.HIGHEST
    direct_list = []
    mirror_list = []
    for matrix in (matrix_sat, matrix_ter):
        masked_upper = jnp.where(upper_mask, matrix, 0.0)
        masked_strict = jnp.where(strict_mask, matrix, 0.0)
        direct_list.append(
            lax.dot_general(probes, masked_upper, (((1,), (1,)), ((), ())), precision=hp)
        )
        mirror_list.append(jnp.dot(slab_probes, masked_strict, precision=hp))
    direct_terms = jnp.stack(direct_list)
    mirror_terms = jnp.stack(mirror_list)
    early_local = jnp.sum(slab_probes[None] * direct_terms, axis=2) + jnp.sum(
        probes[None] * mirror_terms, axis=2
    )
    early_trace = lax.psum(early_local, ("blk", "grp"))
    row_part = lax.psum(direct_terms, "blk")
    column_part = lax.psum_scatter(mirror_terms, "grp", scatter_dimension=2, tiled=True)
    return (row_part, column_part, early_trace)


def solution(mesh):
    in_specs = (P("grp", "blk"), P("grp", "blk"), P(None, "blk"))
    out_specs = (P(None, None, "grp"), P(None, None, ("blk", "grp")), P())
    return jax.shard_map(shards, mesh=mesh, in_specs=in_specs, out_specs=out_specs, check_vma=False)
```

profile of v0, /device:TPU:14, one launch (start us, length us, event | category | flops | bytes accessed | tf_op | source)
XLA Modules:
  0.0 133.0 jit_solution(6201908092485074033)
XLA Ops:
  7.2 0.0 copy-start.2
  7.2 0.0 reduce-scatter.2.cloned.1.call-start
  7.2 0.0 copy-start
  7.3 5.8 %fusion.14 = f32[1,16,256]{2,1,0:T(8,128)S(1)} fusion(f32[16,4096]{1,0:T(8,128)} %param.5, f32[256,4096]{1,0:T(8,128)} %param.4, s32[4096]{0:T(1024)S(1)} %iota_add_fusion, s32[256]{0:T(256)S(1)} %iota_add_fusion.1), kind=kOutput, calls=%fused_computation.20 | convolution fusion | flops 203423744 | bytes 4490240 | tf_op jit(solution)/shard_map/dot_general | solution.py:29
  13.1 0.0 copy-done.2
  13.1 0.0 copy-done
  13.1 3.5 %fusion.15 = f32[1,16,256]{2,1,0:T(8,128)S(1)} fusion(f32[16,4096]{1,0:T(8,128)S(1)} %copy-done.2, f32[256,4096]{1,0:T(8,128)S(1)} %copy-done, s32[4096]{0:T(1024)S(1)} %iota_add_fusion, s32[256]{0:T(256)S(1)} %iota_add_fusion.1), kind=kOutput, calls=%fused_computation.21 | convolution fusion | flops 203423744 | bytes 4490240 | tf_op jit(solution)/shard_map/dot_general | solution.py:29
  16.6 49.1 %all-reduce = (f32[2,16,256]{2,1,0:T(8,128)}, f32[16,256]{1,0:T(8,128)S(1)}) all-reduce(f32[2,16,256]{2,1,0:T(8,128)S(1)} %pad_maximum_fusion.1, f32[16,256]{1,0:T(8,128)S(1)} %dynamic-slice_select_fusion), channel_id=1, replica_groups=mesh['blk'=16,'grp'=2] {'blk'}, use_global_device_ids=true, to_apply=%region_0.1 | all-reduce | flops 12288 | bytes 98304 | tf_op jit(solution)/shard_map/psum | solution.py:38
  65.7 0.0 copy-start.1
  65.7 4.7 %convolution_bitcast_fusion = f32[1,16,4096]{2,1,0:T(8,128)S(1)} fusion(f32[16,256]{1,0:T(8,128)S(1)} %get-tuple-element.4, f32[256,4096]{1,0:T(8,128)} %param.4, s32[4096]{0:T(1024)S(1)} %iota_add_fusion, s32[256]{0:T(256)S(1)} %iota_add_fusion.1), kind=kOutput, calls=%fused_computation.4 | convolution fusion | flops 203423744 | bytes 4490240 | tf_op jit(solution)/shard_map/dot_general | solution.py:31
  70.4 0.0 copy-done.1
  70.4 2.4 %convolution_bitcast_fusion.1 = f32[1,16,4096]{2,1,0:T(8,128)S(1)} fusion(f32[16,256]{1,0:T(8,128)S(1)} %get-tuple-element.4, f32[256,4096]{1,0:T(8,128)S(1)} %copy-done.1, s32[4096]{0:T(1024)S(1)} %iota_add_fusion, s32[256]{0:T(256)S(1)} %iota_add_fusion.1), kind=kOutput, calls=%fused_computation.5 | convolution fusion | flops 203423744 | bytes 4490240 | tf_op jit(solution)/shard_map/dot_general | solution.py:31
  72.8 0.9 multiply_reduce_fusion
  73.7 0.0 reduce-scatter.2.cloned.1.call-update
  73.7 0.1 multiply_reduce_fusion.1
  73.8 52.4 %psum.23 = f32[2,16]{1,0:T(2,128)} all-reduce(f32[2,16]{1,0:T(2,128)S(1)} %add.33), channel_id=1, replica_groups=mesh['blk'=16,'grp'=2] {'blk','grp'}, use_global_device_ids=true, to_apply=%region_5.6 | all-reduce | flops 32 | bytes 256 | tf_op jit(solution)/shard_map/psum | solution.py:37
  126.2 0.0 reduce-scatter.2.cloned.1.call-done
  (5 shorter events, 0.0 us)
Async XLA Ops:
  7.2 5.9 %copy-start.2 = (f32[16,4096]{1,0:T(8,128)S(1)}, f32[16,4096]{1,0:T(8,128)}, u32[]{:S(2)}) copy-start(f32[16,4096]{1,0:T(8,128)} %param.5) | copy-start | bytes 786436
  7.2 119.0 %reduce-scatter.2.cloned.1.call-start = ((), (), s32[]{:S(2)}) async-start(), calls=%async_computation.1 | async-start | bytes 786432 | tf_op jit(solution)/shard_map/reduce_scatter | solution.py:39
  7.2 5.9 %copy-start = (f32[256,4096]{1,0:T(8,128)S(1)}, f32[256,4096]{1,0:T(8,128)}, u32[]{:S(2)}) copy-start(f32[256,4096]{1,0:T(8,128)} %param.3) | copy-start | bytes 12582916
  65.7 4.7 %copy-start.1 = (f32[256,4096]{1,0:T(8,128)S(1)}, f32[256,4096]{1,0:T(8,128)}, u32[]{:S(2)}) copy-start(f32[256,4096]{1,0:T(8,128)} %param.3) | copy-start | bytes 12582916
Sparse Core Ops, SparseCore 0:
  73.8 24.2 reduce-scatter.1
where the time goes:
time: 133 us
  blocking collectives  101 us (76%)
  matrix products  16.3 us (12%)
  between operations  14.1 us (11%)
    psum x1, blocking collectives, shards(): early_trace = lax.psum(early_local, ('blk', 'grp'))  52.4 us
    psum x1, blocking collectives, shards(): row_part = lax.psum(direct_terms, 'blk')  49.1 us
    dot_general x2, matrix products, shards(): lax.dot_general(probes, masked_upper, (((1,), (1,)), ((), ())), precision...  9.25 us
    dot_general x2, matrix products, shards(): mirror_list.append(jnp.dot(slab_probes, masked_strict, precision=hp))  7.08 us
  transfers between devices with their start and end apart: 1, of which 0 were waited for; matrix products, arithmetic and copies ran while one was open for 0% of the time, Pallas kernels for 0%

commit v1 on v0

--- a/solution.py
+++ b/solution.py
@@ -2,6 +2,7 @@
 import jax.numpy as jnp
 from jax import lax
 from jax.sharding import PartitionSpec as P
+from jax.lax import ppermute, psum
 
 
 def broadcast(block, axis, source):
@@ -10,6 +11,25 @@
 
 
 def shards(matrix_sat, matrix_ter, probes):
+
+    def _refer_loops(field, mesh_name):
+        k_all = psum(1, axis_name=mesh_name)
+
+        def bind_ends(all_rows, newest):
+            if newest >= k_all:
+                return all_rows
+            return bind_ends(
+                all_rows
+                + ppermute(
+                    all_rows,
+                    axis_name=mesh_name,
+                    perm=tuple(((p, p ^ newest) for p in range(k_all))),
+                ),
+                2 * newest,
+            )
+
+        return bind_ends(field, 1)
+
     rows_dev, cols_dev = matrix_sat.shape
     column_index = lax.axis_index("blk")
     row_index = lax.axis_index("grp")
@@ -35,7 +55,7 @@
         probes[None] * mirror_terms, axis=2
     )
     early_trace = lax.psum(early_local, ("blk", "grp"))
-    row_part = lax.psum(direct_terms, "blk")
+    row_part = _refer_loops(direct_terms, "blk")
     column_part = lax.psum_scatter(mirror_terms, "grp", scatter_dimension=2, tiled=True)
     return (row_part, column_part, early_trace)
 

time: 133 us -> 145 us (1.090); the launches traced: 133 us -> 143 us
  starting transfers between devices: 0.04 us -> 14.2 us
  blocking collectives: 101 us -> 90.6 us
  waiting for transfers between devices: 0.02 us -> 5 us
    ppermute x0 -> x4, starting transfers between devices: none -> 14.2 us  [bind_ends(): ppermute(all_rows, axis_name=mesh_name, perm=tuple(((p, p ^ newest) for p...]
    psum x1, blocking collectives: 52.4 us -> 41.6 us  [shards(): early_trace = lax.psum(early_local, ('blk', 'grp'))]
    ppermute x0 -> x4, waiting for transfers between devices: none -> 4.98 us  [bind_ends(): ppermute(all_rows, axis_name=mesh_name, perm=tuple(((p, p ^ newest) for p...]
  transfers between devices with their start and end apart: 1 -> 5, of which waited for: 0 -> 3; matrix products, arithmetic and copies ran while one was open for 0% -> 7% of each run, Pallas kernels for 0% -> 0%
where the time goes in v1:
time: 145 us; the launch traced here: 143 us
  blocking collectives  90.6 us (62%)
  matrix products  16.3 us (11%)
  starting transfers between devices  14.2 us (10%)
  between operations  14.1 us (10%)
  waiting for transfers between devices  5 us (3%)
  other arithmetic  2.34 us (2%)
    psum x1, blocking collectives, broadcast(): return lax.psum(block, axis)  49 us
    psum x1, blocking collectives, shards(): early_trace = lax.psum(early_local, ('blk', 'grp'))  41.6 us
    ppermute x4, starting transfers between devices, bind_ends(): ppermute(all_rows, axis_name=mesh_name, perm=tuple(((p, p ^ newest) for p...  14.2 us
    dot_general x2, matrix products, shards(): lax.dot_general(probes, masked_upper, (((1,), (1,)), ((), ())), precision...  9.23 us
    dot_general x2, matrix products, shards(): mirror_list.append(jnp.dot(slab_probes, masked_strict, precision=hp))  7.08 us
    ppermute x4, waiting for transfers between devices, bind_ends(): ppermute(all_rows, axis_name=mesh_name, perm=tuple(((p, p ^ newest) for p...  4.98 us
  transfers between devices with their start and end apart: 5, of which 3 were waited for; matrix products, arithmetic and copies ran while one was open for 7% of the time, Pallas kernels for 0%

profile of v1, /device:TPU:14, one launch (start us, length us, event | category | flops | bytes accessed | tf_op | source)
XLA Modules:
  0.0 142.6 jit_solution(14861866257701781627)
XLA Ops:
  7.2 0.0 reduce-scatter.2.cloned.1.call-start
  7.2 0.7 dynamic-slice_select_fusion
  8.0 49.0 %psum.14 = f32[16,256]{1,0:T(8,128)S(1)} all-reduce(f32[16,256]{1,0:T(8,128)S(1)} %dynamic-slice_select_fusion), channel_id=1, replica_groups=mesh['blk'=16,'grp'=2] {'blk'}, use_global_device_ids=true, to_apply=%region_0.1 | all-reduce | flops 4096 | bytes 32768 | tf_op jit(solution)/shard_map/psum | solution.py:10
  57.0 0.0 copy-start
  57.0 0.0 copy-start.2
  57.0 4.7 %convolution_bitcast_fusion.1 = f32[1,16,4096]{2,1,0:T(8,128)S(1)} fusion(f32[16,256]{1,0:T(8,128)S(1)} %psum.14, f32[256,4096]{1,0:T(8,128)} %param.3, s32[4096]{0:T(1024)S(1)} %iota_add_fusion, s32[256]{0:T(256)S(1)} %iota_add_fusion.1), kind=kOutput, calls=%fused_computation.5 | convolution fusion | flops 203423744 | bytes 4490240 | tf_op jit(solution)/shard_map/dot_general | solution.py:51
  61.7 0.0 copy-done
  61.7 2.4 %convolution_bitcast_fusion = f32[1,16,4096]{2,1,0:T(8,128)S(1)} fusion(f32[16,256]{1,0:T(8,128)S(1)} %psum.14, f32[256,4096]{1,0:T(8,128)S(1)} %copy-done, s32[4096]{0:T(1024)S(1)} %iota_add_fusion, s32[256]{0:T(256)S(1)} %iota_add_fusion.1), kind=kOutput, calls=%fused_computation.4 | convolution fusion | flops 203423744 | bytes 4490240 | tf_op jit(solution)/shard_map/dot_general | solution.py:51
  64.1 0.0 copy-done.2
  64.1 0.9 multiply_reduce_fusion
  64.9 0.0 reduce-scatter.2.cloned.1.call-update
  65.0 0.0 copy-start.1
  65.0 5.8 %fusion.14 = f32[1,16,256]{2,1,0:T(8,128)S(1)} fusion(f32[16,4096]{1,0:T(8,128)S(1)} %copy-done.2, f32[256,4096]{1,0:T(8,128)} %param.4, s32[4096]{0:T(1024)S(1)} %iota_add_fusion, s32[256]{0:T(256)S(1)} %iota_add_fusion.1), kind=kOutput, calls=%fused_computation.20 | convolution fusion | flops 203423744 | bytes 4490240 | tf_op jit(solution)/shard_map/dot_general | solution.py:49
  70.7 0.0 copy-done.1
  70.8 3.5 %fusion.15 = f32[1,16,256]{2,1,0:T(8,128)S(1)} fusion(f32[16,4096]{1,0:T(8,128)S(1)} %copy-done.2, f32[256,4096]{1,0:T(8,128)S(1)} %copy-done.1, s32[4096]{0:T(1024)S(1)} %iota_add_fusion, s32[256]{0:T(256)S(1)} %iota_add_fusion.1), kind=kOutput, calls=%fused_computation.21 | convolution fusion | flops 203423744 | bytes 4490240 | tf_op jit(solution)/shard_map/dot_general | solution.py:49
  74.2 0.1 collective-permute-start
  74.3 1.2 collective-permute-done
  75.5 0.1 multiply_reduce_fusion.1
  75.6 5.0 %collective-permute-start.1 = (f32[2,16,256]{2,1,0:T(8,128)S(1)}, f32[2,16,256]{2,1,0:T(8,128)S(1)}, u32[]{:S(2)}, u32[]{:S(2)}) collective-permute-start(f32[2,16,256]{2,1,0:T(8,128)S(1)} %get-tuple-element.6), channel_id=1, source_target_pairs={{0,4},{2,6},{4,0},{6,2},{8,12},{10,14},{12,8},{14,10},{16,20},{18,... | collective-permute-start | bytes 98312 | tf_op jit(solution)/shard_map/ppermute | solution.py:23
  80.6 1.9 %collective-permute-done.1 = f32[2,16,256]{2,1,0:T(8,128)S(1)} collective-permute-done((f32[2,16,256]{2,1,0:T(8,128)S(1)}, f32[2,16,256]{2,1,0:T(8,128)S(1)}, u32[]{:S(2)}, u32[]{:S(2)}) %collective-permute-start.1) | collective-permute-done | bytes 32800 | tf_op jit(solution)/shard_map/ppermute | solution.py:23
  82.5 8.4 %collective-permute-start.2 = (f32[2,16,256]{2,1,0:T(8,128)S(1)}, f32[2,16,256]{2,1,0:T(8,128)S(1)}, u32[]{:S(2)}, u32[]{:S(2)}) collective-permute-start(f32[2,16,256]{2,1,0:T(8,128)S(1)} %add.43), channel_id=1, source_target_pairs={{0,8},{2,10},{4,12},{6,14},{8,0},{10,2},{12,4},{14,6},{16,24},{18,... | collective-permute-start | bytes 98312 | tf_op jit(solution)/shard_map/ppermute | solution.py:23
  90.9 1.9 %collective-permute-done.2 = f32[2,16,256]{2,1,0:T(8,128)S(1)} collective-permute-done((f32[2,16,256]{2,1,0:T(8,128)S(1)}, f32[2,16,256]{2,1,0:T(8,128)S(1)}, u32[]{:S(2)}, u32[]{:S(2)}) %collective-permute-start.2) | collective-permute-done | bytes 32800 | tf_op jit(solution)/shard_map/ppermute | solution.py:23
  92.8 0.6 collective-permute-start.3
  93.5 41.6 %psum.15 = f32[2,16]{1,0:T(2,128)} all-reduce(f32[2,16]{1,0:T(2,128)S(1)} %add.47), channel_id=1, replica_groups=mesh['blk'=16,'grp'=2] {'blk','grp'}, use_global_device_ids=true, to_apply=%region_4.5 | all-reduce | flops 32 | bytes 256 | tf_op jit(solution)/shard_map/psum | solution.py:57
  135.1 0.0 collective-permute-done.3
  135.1 0.6 add.45
  135.7 0.0 reduce-scatter.2.cloned.1.call-done
  (6 shorter events, 0.0 us)
Async XLA Ops:
  7.2 128.5 %reduce-scatter.2.cloned.1.call-start = ((), (), s32[]{:S(2)}) async-start(), calls=%async_computation.1 | async-start | bytes 786432 | tf_op jit(solution)/shard_map/reduce_scatter | solution.py:59
  57.0 4.7 %copy-start = (f32[256,4096]{1,0:T(8,128)S(1)}, f32[256,4096]{1,0:T(8,128)}, u32[]{:S(2)}) copy-start(f32[256,4096]{1,0:T(8,128)} %param.4) | copy-start | bytes 12582916
  57.0 7.1 %copy-start.2 = (f32[16,4096]{1,0:T(8,128)S(1)}, f32[16,4096]{1,0:T(8,128)}, u32[]{:S(2)}) copy-start(f32[16,4096]{1,0:T(8,128)} %param.5) | copy-start | bytes 786436
  65.0 5.8 %copy-start.1 = (f32[256,4096]{1,0:T(8,128)S(1)}, f32[256,4096]{1,0:T(8,128)}, u32[]{:S(2)}) copy-start(f32[256,4096]{1,0:T(8,128)} %param.3) | copy-start | bytes 12582916
  74.2 1.3 collective-permute-start
  75.6 6.9 %collective-permute-start.1 = (f32[2,16,256]{2,1,0:T(8,128)S(1)}, f32[2,16,256]{2,1,0:T(8,128)S(1)}, u32[]{:S(2)}, u32[]{:S(2)}) collective-permute-start(f32[2,16,256]{2,1,0:T(8,128)S(1)} %get-tuple-element.6), channel_id=1, source_target_pairs={{0,4},{2,6},{4,0},{6,2},{8,12},{10,14},{12,8},{14,10},{16,20},{18,... | collective-permute-start | bytes 98312 | tf_op jit(solution)/shard_map/ppermute | solution.py:23
  82.5 10.3 %collective-permute-start.2 = (f32[2,16,256]{2,1,0:T(8,128)S(1)}, f32[2,16,256]{2,1,0:T(8,128)S(1)}, u32[]{:S(2)}, u32[]{:S(2)}) collective-permute-start(f32[2,16,256]{2,1,0:T(8,128)S(1)} %add.43), channel_id=1, source_target_pairs={{0,8},{2,10},{4,12},{6,14},{8,0},{10,2},{12,4},{14,6},{16,24},{18,... | collective-permute-start | bytes 98312 | tf_op jit(solution)/shard_map/ppermute | solution.py:23
  92.8 42.2 %collective-permute-start.3 = (f32[2,16,256]{2,1,0:T(8,128)S(1)}, f32[2,16,256]{2,1,0:T(8,128)S(1)}, u32[]{:S(2)}, u32[]{:S(2)}) collective-permute-start(f32[2,16,256]{2,1,0:T(8,128)S(1)} %add.44), channel_id=1, source_target_pairs={{0,16},{2,18},{4,20},{6,22},{8,24},{10,26},{12,28},{14,30},{16,0},... | collective-permute-start | bytes 98312 | tf_op jit(solution)/shard_map/ppermute | solution.py:23
Sparse Core Ops, SparseCore 0:
  65.1 23.2 reduce-scatter.1

commit v2 on v0

--- a/solution.py
+++ b/solution.py
@@ -34,7 +34,9 @@
     early_local = jnp.sum(slab_probes[None] * direct_terms, axis=2) + jnp.sum(
         probes[None] * mirror_terms, axis=2
     )
-    early_trace = lax.psum(early_local, ("blk", "grp"))
+    early_trace = early_local
+    for name in ("grp", "blk"):
+        early_trace = lax.psum(early_trace, name)
     row_part = lax.psum(direct_terms, "blk")
     column_part = lax.psum_scatter(mirror_terms, "grp", scatter_dimension=2, tiled=True)
     return (row_part, column_part, early_trace)

time: 133 us -> 159 us (1.20)
  the two profiles are of different devices: /device:TPU:14 before, /device:TPU:0 now
where the time goes in v2:
time: 159 us; the launch traced here: 158 us
  blocking collectives  126 us (79%)
  matrix products  16.3 us (10%)
  between operations  14.1 us (9%)
  other arithmetic  1.71 us (1%)
    psum x1, blocking collectives, broadcast(): return lax.psum(block, axis)  63 us
    psum x1, blocking collectives, shards(): row_part = lax.psum(direct_terms, 'blk')  58.3 us
    dot_general x2, matrix products, shards(): lax.dot_general(probes, masked_upper, (((1,), (1,)), ((), ())), precision...  9.23 us
    dot_general x2, matrix products, shards(): mirror_list.append(jnp.dot(slab_probes, masked_strict, precision=hp))  7.08 us
    psum x1, blocking collectives, shards(): early_trace = lax.psum(early_trace, name)  4.92 us
  transfers between devices with their start and end apart: 1, of which 0 were waited for; matrix products, arithmetic and copies ran while one was open for 6% of the time, Pallas kernels for 0%

profile of v2, /device:TPU:0, one launch (start us, length us, event | category | flops | bytes accessed | tf_op | source)
XLA Modules:
  0.0 158.3 jit_solution(5963326211020129214)
XLA Ops:
  7.2 0.0 reduce-scatter.2.cloned.1.call-start
  7.2 0.7 dynamic-slice_select_fusion
  8.0 63.0 %psum.29 = f32[16,256]{1,0:T(8,128)S(1)} all-reduce(f32[16,256]{1,0:T(8,128)S(1)} %dynamic-slice_select_fusion), channel_id=1, replica_groups=mesh['blk'=16,'grp'=2] {'blk'}, use_global_device_ids=true, to_apply=%region_1.2 | all-reduce | flops 4096 | bytes 32768 | tf_op jit(solution)/shard_map/psum | solution.py:9
  70.9 0.0 copy-start
  70.9 0.0 copy-start.2
  70.9 4.7 %convolution_bitcast_fusion.1 = f32[1,16,4096]{2,1,0:T(8,128)S(1)} fusion(f32[16,256]{1,0:T(8,128)S(1)} %psum.29, f32[256,4096]{1,0:T(8,128)} %param.3, s32[4096]{0:T(1024)S(1)} %iota_add_fusion, s32[256]{0:T(256)S(1)} %iota_add_fusion.1), kind=kOutput, calls=%fused_computation.5 | convolution fusion | flops 203423744 | bytes 4490240 | tf_op jit(solution)/shard_map/dot_general | solution.py:31
  75.7 0.0 copy-done
  75.7 2.4 %convolution_bitcast_fusion = f32[1,16,4096]{2,1,0:T(8,128)S(1)} fusion(f32[16,256]{1,0:T(8,128)S(1)} %psum.29, f32[256,4096]{1,0:T(8,128)S(1)} %copy-done, s32[4096]{0:T(1024)S(1)} %iota_add_fusion, s32[256]{0:T(256)S(1)} %iota_add_fusion.1), kind=kOutput, calls=%fused_computation.4 | convolution fusion | flops 203423744 | bytes 4490240 | tf_op jit(solution)/shard_map/dot_general | solution.py:31
  78.0 0.0 copy-done.2
  78.0 0.9 pad_maximum_fusion
  78.9 0.0 reduce-scatter.2.cloned.1.call-update
  78.9 0.0 copy-start.1
  78.9 5.8 %fusion.14 = f32[1,16,256]{2,1,0:T(8,128)S(1)} fusion(f32[16,4096]{1,0:T(8,128)S(1)} %copy-done.2, f32[256,4096]{1,0:T(8,128)} %param.4, s32[4096]{0:T(1024)S(1)} %iota_add_fusion, s32[256]{0:T(256)S(1)} %iota_add_fusion.1), kind=kOutput, calls=%fused_computation.20 | convolution fusion | flops 203423744 | bytes 4490240 | tf_op jit(solution)/shard_map/dot_general | solution.py:29
  84.7 0.0 copy-done.1
  84.7 3.5 %fusion.15 = f32[1,16,256]{2,1,0:T(8,128)S(1)} fusion(f32[16,4096]{1,0:T(8,128)S(1)} %copy-done.2, f32[256,4096]{1,0:T(8,128)S(1)} %copy-done.1, s32[4096]{0:T(1024)S(1)} %iota_add_fusion, s32[256]{0:T(256)S(1)} %iota_add_fusion.1), kind=kOutput, calls=%fused_computation.21 | convolution fusion | flops 203423744 | bytes 4490240 | tf_op jit(solution)/shard_map/dot_general | solution.py:29
  88.2 0.1 multiply_reduce_fusion.1
  88.3 4.9 %psum.30 = f32[2,16]{1,0:T(2,128)S(1)} all-reduce(f32[2,16]{1,0:T(2,128)S(1)} %add.35), channel_id=1, replica_groups=mesh['blk'=16,'grp'=2] {'grp'}, use_global_device_ids=true, to_apply=%region_5.6 | all-reduce | flops 32 | bytes 256 | tf_op jit(solution)/shard_map/psum | solution.py:39
  93.2 58.3 %all-reduce = (f32[2,16,256]{2,1,0:T(8,128)}, f32[2,16]{1,0:T(2,128)}) all-reduce(f32[2,16,256]{2,1,0:T(8,128)S(1)} %get-tuple-element.8, f32[2,16]{1,0:T(2,128)S(1)} %psum.30), channel_id=1, replica_groups=mesh['blk'=16,'grp'=2] {'blk'}, use_global_device_ids=true, to_apply=%region_0.1 | all-reduce | flops 8224 | bytes 65792 | tf_op jit(solution)/shard_map/psum | solution.py:40
  151.5 0.0 reduce-scatter.2.cloned.1.call-done
  (3 shorter events, 0.0 us)
Async XLA Ops:
  7.2 144.3 %reduce-scatter.2.cloned.1.call-start = ((), (), s32[]{:S(2)}) async-start(), calls=%async_computation.1 | async-start | bytes 786432 | tf_op jit(solution)/shard_map/reduce_scatter | solution.py:41
  70.9 4.7 %copy-start = (f32[256,4096]{1,0:T(8,128)S(1)}, f32[256,4096]{1,0:T(8,128)}, u32[]{:S(2)}) copy-start(f32[256,4096]{1,0:T(8,128)} %param.4) | copy-start | bytes 12582916
  70.9 7.1 %copy-start.2 = (f32[16,4096]{1,0:T(8,128)S(1)}, f32[16,4096]{1,0:T(8,128)}, u32[]{:S(2)}) copy-start(f32[16,4096]{1,0:T(8,128)} %param.5) | copy-start | bytes 786436
  78.9 5.8 %copy-start.1 = (f32[256,4096]{1,0:T(8,128)S(1)}, f32[256,4096]{1,0:T(8,128)}, u32[]{:S(2)}) copy-start(f32[256,4096]{1,0:T(8,128)} %param.3) | copy-start | bytes 12582916
Sparse Core Ops, SparseCore 0:
  79.0 11.9 reduce-scatter.1
